TPU v7x, 256 devices: a 2x2x32 block of a 4x8x32 slice. The times are simulated.
256 devices in a mesh: group: 4 (over y, x), blk: 64 (over z, core).
Axes of the slice: x: 2, y: 2, z: 32, core: 2. Of those that a mesh axis runs over, the one named last changes fastest.
The devices are a block of a 4x8x32 slice.
Arguments:
- queries: bfloat16 [8, 256, 2048], P('group', 'blk'), parts along dimension 0, may hold values from -160 to 160
- keys: bfloat16 [8, 81920, 256], P('group', 'blk'), parts along dimension 0, may hold values from -4 to 4
- values: bfloat16 [8, 81920, 256], P('group', 'blk'), parts along dimension 0, may hold values from -6 to 6
- lengths: int32 [8], P('group'), parts along dimension 0, may hold values from 61440 to 81920
- offsets: int32 [8], P('group'), parts along dimension 0, may hold values from 51200 to 81664
Outputs:
- attended: bfloat16 [8, 256, 2048], P('group', 'blk'), parts along dimension 0
There are 4 independent parts, one for each index of `group`. A program takes and returns all parts, laid end to end along the dimension named above; each array names one. Nothing has to cross between parts.
All inputs are finite; a program needn't handle non-finite values.
Results may differ from a plain program's by a relative error of at most 0.0085.
Values may be sent and summed in bfloat16 or wider, within the bound.
A program may use at most 64 MiB of HBM per device.

v0:
```python
import math
import jax
import jax.numpy as jnp
from jax import lax
from jax.sharding import PartitionSpec as P

KV_HEADS = 2
HEAD_DIM = 128
masked_low = -1e30


def shard_partial(query_rows, key_rows, value_rows, query_pos, key_pos, lengths):
    micro_count, rows_count, row_width = query_rows.shape
    heads_count = row_width // HEAD_DIM
    group_size = heads_count // KV_HEADS
    query_split = query_rows.reshape(micro_count, rows_count, KV_HEADS, group_size, HEAD_DIM)
    key_split = key_rows.reshape(micro_count, key_rows.shape[1], KV_HEADS, HEAD_DIM)
    value_split = value_rows.reshape(micro_count, value_rows.shape[1], KV_HEADS, HEAD_DIM)
    scores = jnp.einsum(
        "brkgd,bskd->bkgrs", query_split, key_split, preferred_element_type=jnp.float32
    )
    scores = scores * (1.0 / math.sqrt(HEAD_DIM))
    visible = (key_pos[None, None, :] <= query_pos[:, :, None]) & (
        key_pos[None, None, :] < lengths[:, None, None]
    )
    visible = visible[:, None, None, :, :]
    any_visible = jnp.any(visible, axis=-1)
    row_max = jnp.max(jnp.where(visible, scores, masked_low), axis=-1)
    safe_max = jnp.where(any_visible, row_max, 0.0)
    shifted = jnp.where(visible, scores - safe_max[..., None], 0.0)
    weights = jnp.where(visible, jnp.exp(shifted), 0.0)
    totals = jnp.sum(weights, axis=-1)
    bounded = jnp.maximum(totals, 1.0)
    numerator = jnp.einsum(
        "bkgrs,bskd->bkgrd",
        weights.astype(jnp.bfloat16),
        value_split,
        preferred_element_type=jnp.float32,
    )
    partial_value = (numerator / bounded[..., None]).astype(jnp.bfloat16)
    partial_value = jnp.transpose(partial_value, (0, 3, 1, 2, 4)).reshape(
        micro_count, rows_count, row_width
    )
    logsum = jnp.where(any_visible, safe_max + jnp.log(bounded), masked_low)
    logsum = jnp.transpose(logsum, (0, 3, 1, 2)).reshape(micro_count, rows_count, heads_count)
    return (partial_value, logsum)


def body(queries, keys, values, lengths, offsets):
    micro_count, local_rows, row_width = queries.shape
    local_keys = keys.shape[1]
    heads_count = row_width // HEAD_DIM
    shards = lax.axis_size("blk")
    key_pos = lax.axis_index("blk") * local_keys + jnp.arange(local_keys, dtype=jnp.int32)
    visiting = lax.all_gather(queries, "blk", axis=1, tiled=True)
    rows_count = visiting.shape[1]
    block_rows = math.gcd(rows_count, 64)
    block_count = rows_count // block_rows

    def one_block(block_index):
        block_start = block_index * block_rows
        selected = lax.dynamic_slice_in_dim(visiting, block_start, block_rows, 1)
        query_pos = (
            offsets[:, None] + block_start + jnp.arange(block_rows, dtype=jnp.int32)[None, :]
        )
        return shard_partial(selected, keys, values, query_pos, key_pos, lengths)

    block_parts, block_logs = lax.map(one_block, jnp.arange(block_count, dtype=jnp.int32))
    block_parts = jnp.moveaxis(block_parts, 0, 1).reshape(micro_count, rows_count, row_width)
    block_logs = jnp.moveaxis(block_logs, 0, 1).reshape(micro_count, rows_count, heads_count)
    partials = block_parts
    logsums = block_logs
    partials, logsums = (partials, logsums)
    shaped_parts = partials.reshape(micro_count, shards, local_rows, row_width)
    shaped_logs = logsums.reshape(micro_count, shards, local_rows, heads_count)
    home_parts = lax.all_to_all(shaped_parts, "blk", split_axis=1, concat_axis=1, tiled=True)
    home_logs = lax.all_to_all(shaped_logs, "blk", split_axis=1, concat_axis=1, tiled=True)
    row_peak = jnp.max(home_logs, axis=1, keepdims=True)
    scales = jnp.exp(home_logs - row_peak)
    denominator = jnp.sum(scales, axis=1)
    split_parts = home_parts.reshape(micro_count, shards, local_rows, heads_count, HEAD_DIM)
    weighted = jnp.sum(split_parts * scales[..., None], axis=1)
    merged = weighted / denominator[..., None]
    attended = merged.reshape(micro_count, local_rows, row_width).astype(jnp.bfloat16)
    return attended


def solution(mesh):
    return jax.shard_map(
        body,
        mesh=mesh,
        in_specs=(
            P("group", "blk", None),
            P("group", "blk", None),
            P("group", "blk", None),
            P("group"),
            P("group"),
        ),
        out_specs=P("group", "blk", None),
        check_vma=False,
    )
```

profile of v0, /device:TPU:37, one launch (start us, length us, event | category | flops | bytes accessed | tf_op | source)
XLA Modules:
  0.0 481.0 jit_solution(16185152529671269494)
XLA Ops:
  6.6 1.4 copy.51
  8.1 3.8 reshape.97
  11.9 2.9 reshape.98
  14.9 139.4 %all-gather.2.cloned.1.call-done = bf16[2,256,2048]{2,0,1:T(2,128)(2,1)} async-done(((bf16[2,4,2048]{2,0,1:T(2,128)(2,1)}), bf16[2,256,2048]{2,0,1:T(2,128)(2,1)}) %all-gather.2.cloned.1.call-update) | async-done | bytes 2097168 | tf_op jit(solution)/shard_map/all_gather | solution.py:55
  154.3 71.4 %while.14 = (s32[]{:T(128)}, bf16[4,2,64,2048]{3,2,1,0:T(8,128)(2,1)}, f32[4,2,64,16]{2,3,1,0:T(8,128)S(1)}, s32[4]{0:T(128)S(1)}, s32[2]{0:T(128)S(1)}, /*index...) while((s32[]{:T(128)}, ...), condition=%wide.wide.region_4.5_spmd.clone, body=%wide.wide.region_0.4_spmd.clone.sunk | while | flops 1377611520 | bytes 88389816 | solution.py:68
  155.5 1.4 constant_dynamic-slice_fusion.3
  157.6 3.0 fusion.38
  161.0 4.3 fusion.39
  165.5 5.4 %divide_convert_fusion.4 = bf16[2,64,2,8,128]{4,3,1,2,0:T(8,128)(2,1)S(1)} fusion(bf16[2,1280,2,128,1]{3,2,1,0,4:T(2,128)(2,1)S(1)} %bitcast.95, f32[2,2,64,8,1280]{4,3,2,1,0:T(8,128)} %copy-done, f32[2,2,8,64]{2,3,1,0:T(8,128)S(1)} %broadcast_select_fusion.3, pred[2,64,1280]{2,1,0:T(8,128)(4,1)S(1)} %compare_and_fusion.3, ...), kind=kOutput, calls=%fused_computation.15.clone.clone.1 | convolution fusion | flops 684720128 | bytes 12500992 | tf_op jit(solution)/shard_map/while/body/eval_jaxpr/bkgrs,bskd->bkgrd/dot_general | solution.py:34
  171.3 0.9 constant_dynamic-update-slice_fusion.3
  173.4 1.4 constant_dynamic-slice_fusion.3
  175.5 3.0 fusion.38
  178.8 4.3 fusion.39
  183.4 5.4 %divide_convert_fusion.4 = bf16[2,64,2,8,128]{4,3,1,2,0:T(8,128)(2,1)S(1)} fusion(bf16[2,1280,2,128,1]{3,2,1,0,4:T(2,128)(2,1)S(1)} %bitcast.95, f32[2,2,64,8,1280]{4,3,2,1,0:T(8,128)} %copy-done, f32[2,2,8,64]{2,3,1,0:T(8,128)S(1)} %broadcast_select_fusion.3, pred[2,64,1280]{2,1,0:T(8,128)(4,1)S(1)} %compare_and_fusion.3, ...), kind=kOutput, calls=%fused_computation.15.clone.clone.1 | convolution fusion | flops 684720128 | bytes 12500992 | tf_op jit(solution)/shard_map/while/body/eval_jaxpr/bkgrs,bskd->bkgrd/dot_general | solution.py:34
  189.1 0.9 constant_dynamic-update-slice_fusion.3
  191.3 1.4 constant_dynamic-slice_fusion.3
  193.4 3.0 fusion.38
  196.7 4.3 fusion.39
  201.3 5.4 %divide_convert_fusion.4 = bf16[2,64,2,8,128]{4,3,1,2,0:T(8,128)(2,1)S(1)} fusion(bf16[2,1280,2,128,1]{3,2,1,0,4:T(2,128)(2,1)S(1)} %bitcast.95, f32[2,2,64,8,1280]{4,3,2,1,0:T(8,128)} %copy-done, f32[2,2,8,64]{2,3,1,0:T(8,128)S(1)} %broadcast_select_fusion.3, pred[2,64,1280]{2,1,0:T(8,128)(4,1)S(1)} %compare_and_fusion.3, ...), kind=kOutput, calls=%fused_computation.15.clone.clone.1 | convolution fusion | flops 684720128 | bytes 12500992 | tf_op jit(solution)/shard_map/while/body/eval_jaxpr/bkgrs,bskd->bkgrd/dot_general | solution.py:34
  209.1 1.4 constant_dynamic-slice_fusion.3
  211.2 3.0 fusion.38
  214.5 4.3 fusion.39
  219.1 5.4 %divide_convert_fusion.4 = bf16[2,64,2,8,128]{4,3,1,2,0:T(8,128)(2,1)S(1)} fusion(bf16[2,1280,2,128,1]{3,2,1,0,4:T(2,128)(2,1)S(1)} %bitcast.95, f32[2,2,64,8,1280]{4,3,2,1,0:T(8,128)} %copy-done, f32[2,2,8,64]{2,3,1,0:T(8,128)S(1)} %broadcast_select_fusion.3, pred[2,64,1280]{2,1,0:T(8,128)(4,1)S(1)} %compare_and_fusion.3, ...), kind=kOutput, calls=%fused_computation.15.clone.clone.1 | convolution fusion | flops 684720128 | bytes 12500992 | tf_op jit(solution)/shard_map/while/body/eval_jaxpr/bkgrs,bskd->bkgrd/dot_general | solution.py:34
  224.8 0.8 constant_dynamic-update-slice_fusion.3
  226.7 13.8 %all-to-all-start.1 = ((f32[64,1,128]{2,1,0:T(1,128)}), f32[64,1,128]{2,1,0:T(1,128)S(1)}, u32[]{:S(2)}, u32[]{:S(2)}) async-start(f32[64,1,128]{2,1,0:T(1,128)} %reshape.95), calls=%async_computation.1 | async-start | bytes 65536 | tf_op jit(solution)/shard_map/all_to_all | solution.py:77
  240.5 5.1 %copy.53 = bf16[2,4,64,2048]{3,0,2,1:T(2,128)(2,1)} copy(bf16[2,4,64,2048]{3,2,0,1:T(8,128)(2,1)} %bitcast.94) | data formatting | bytes 4194304 | tf_op jit(solution)/shard_map/transpose | solution.py:69
  245.6 16.6 %all-to-all-done.1 = f32[64,1,128]{2,1,0:T(1,128)S(1)} async-done(((f32[64,1,128]{2,1,0:T(1,128)}), f32[64,1,128]{2,1,0:T(1,128)S(1)}, u32[]{:S(2)}, u32[]{:S(2)}) %all-to-all-start.1) | async-done | bytes 32800 | tf_op jit(solution)/shard_map/all_to_all | solution.py:77
  262.2 6.6 %all-to-all-start = ((bf16[2,64,4,2048]{3,0,2,1:T(2,128)(2,1)}), bf16[2,64,4,2048]{3,0,2,1:T(2,128)(2,1)S(1)}, u32[]{:S(2)}, u32[]{:S(2)}) async-start(bf16[2,64,4,2048]{3,0,2,1:T(2,128)(2,1)} %bitcast.93), calls=%async_computation | async-start | bytes 4194304 | tf_op jit(solution)/shard_map/all_to_all | solution.py:76
  270.7 2.6 mul.27
  273.3 5.8 %mul.28 = f32[2,64,4,2048]{3,0,2,1:T(2,128)} reshape(f32[2,64,4,16,128]{4,3,0,2,1:T(8,128)} %mul.27) | data formatting | bytes 8388608 | tf_op jit(solution)/shard_map/mul | solution.py:82
  279.2 189.7 %all-to-all-done = bf16[2,64,4,2048]{3,0,2,1:T(2,128)(2,1)S(1)} async-done(((bf16[2,64,4,2048]{3,0,2,1:T(2,128)(2,1)}), bf16[2,64,4,2048]{3,0,2,1:T(2,128)(2,1)S(1)}, u32[]{:S(2)}, u32[]{:S(2)}) %all-to-all-start) | async-done | bytes 2097184 | tf_op jit(solution)/shard_map/all_to_all | solution.py:76
  468.9 4.5 multiply_reduce_fusion
  (100 shorter events, 13.0 us)
Async XLA Ops:
  6.5 147.7 %copy-start.2 = (s32[2]{0:T(128)S(1)}, s32[2]{0:T(128)}, u32[]{:S(2)}) copy-start(s32[2]{0:T(128)} %param.10) | copy-start | bytes 28
  6.5 147.7 %copy-start.3 = (s32[2]{0:T(128)S(1)}, s32[2]{0:T(128)}, u32[]{:S(2)}) copy-start(s32[2]{0:T(128)} %param.11) | copy-start | bytes 28
  6.6 147.7 %all-gather.2.cloned.1.call-start = ((), (), s32[]{:S(2)}) async-start(), calls=%async_computation.2 | async-start | bytes 2129920 | tf_op jit(solution)/shard_map/all_gather | solution.py:55
  160.6 4.7 copy-start
  161.0 4.5 copy-start.1
  178.5 4.7 copy-start
  178.8 4.5 copy-start.1
  196.3 4.7 copy-start
  196.7 4.5 copy-start.1
  214.2 4.7 copy-start
  214.5 4.5 copy-start.1
  226.7 35.6 %all-to-all-start.1 = ((f32[64,1,128]{2,1,0:T(1,128)}), f32[64,1,128]{2,1,0:T(1,128)S(1)}, u32[]{:S(2)}, u32[]{:S(2)}) async-start(f32[64,1,128]{2,1,0:T(1,128)} %reshape.95), calls=%async_computation.1 | async-start | bytes 65536 | tf_op jit(solution)/shard_map/all_to_all | solution.py:77
  262.2 206.7 %all-to-all-start = ((bf16[2,64,4,2048]{3,0,2,1:T(2,128)(2,1)}), bf16[2,64,4,2048]{3,0,2,1:T(2,128)(2,1)S(1)}, u32[]{:S(2)}, u32[]{:S(2)}) async-start(bf16[2,64,4,2048]{3,0,2,1:T(2,128)(2,1)} %bitcast.93), calls=%async_computation | async-start | bytes 4194304 | tf_op jit(solution)/shard_map/all_to_all | solution.py:76
Sparse Core Ops, SparseCore 0:
  9.2 145.0 all-gather.1
where the time goes:
time: 482 us; the launch traced here: 481 us
  waiting for transfers between devices  346 us (72%)
  local copies, waits for them, and re-layouts  38.7 us (8%)
  matrix products  33.6 us (7%)
  other arithmetic  26 us (5%)
  starting transfers between devices  20.4 us (4%)
  between operations  13.5 us (3%)
    all_to_all x1, waiting for transfers between devices, body(): lax.all_to_all(shaped_parts, 'blk', split_axis=1, concat_axis=1, tiled=True)  190 us
    all_gather x1, waiting for transfers between devices, body(): visiting = lax.all_gather(queries, 'blk', axis=1, tiled=True)  139 us
    dot_general x4, matrix products, shard_partial(): jnp.einsum('bkgrs,bskd->bkgrd', weights.astype(jnp.bfloat16), value_split...  21.7 us
    reduce_sum x4, other arithmetic, shard_partial(): totals = jnp.sum(weights, axis=-1)  17.2 us
    all_to_all x1, waiting for transfers between devices, body(): lax.all_to_all(shaped_logs, 'blk', split_axis=1, concat_axis=1, tiled=True)  16.6 us
    all_to_all x1, starting transfers between devices, body(): lax.all_to_all(shaped_logs, 'blk', split_axis=1, concat_axis=1, tiled=True)  13.8 us
    dot_general x4, matrix products, shard_partial(): jnp.einsum('brkgd,bskd->bkgrs', query_split, key_split, preferred_element...  11.8 us
  transfers between devices with their start and end apart: 3, of which 3 were waited for; matrix products, arithmetic and copies ran while one was open for 5% of the time, Pallas kernels for 0%

commit v1 on v0

--- a/solution.py
+++ b/solution.py
@@ -7,6 +7,14 @@
 KV_HEADS = 2
 HEAD_DIM = 128
 masked_low = -1e30
+
+
+def tiled_gather(array, axis, dim):
+    size = lax.axis_size(axis)
+    repeats = [size if d == dim else 1 for d in range(array.ndim)]
+    return lax.all_to_all(
+        jnp.tile(array, repeats), axis, split_axis=dim, concat_axis=dim, tiled=True
+    )
 
 
 def shard_partial(query_rows, key_rows, value_rows, query_pos, key_pos, lengths):
@@ -52,7 +60,7 @@
     heads_count = row_width // HEAD_DIM
     shards = lax.axis_size("blk")
     key_pos = lax.axis_index("blk") * local_keys + jnp.arange(local_keys, dtype=jnp.int32)
-    visiting = lax.all_gather(queries, "blk", axis=1, tiled=True)
+    visiting = tiled_gather(queries, "blk", 1)
     rows_count = visiting.shape[1]
     block_rows = math.gcd(rows_count, 64)
     block_count = rows_count // block_rows

time: 482 us -> 551 us (1.14)
  waiting for transfers between devices: 346 us -> 401 us
  starting transfers between devices: 20.4 us -> 48.3 us
  between operations: 13.5 us -> 0.14 us
    all_to_all x0 -> x1, waiting for transfers between devices: none -> 196 us  [tiled_gather(): lax.all_to_all(jnp.tile(array, repeats), axis, split_axis=dim, concat_axi...]
    all_gather x1 -> x0, waiting for transfers between devices: 139 us -> none  [body(): visiting = lax.all_gather(queries, 'blk', axis=1, tiled=True)]
    all_to_all x0 -> x1, starting transfers between devices: none -> 34.5 us  [tiled_gather(): lax.all_to_all(jnp.tile(array, repeats), axis, split_axis=dim, concat_axi...]
    all_to_all x1, starting transfers between devices: 13.8 us -> 7.82 us  [body(): lax.all_to_all(shaped_logs, 'blk', split_axis=1, concat_axis=1, tiled=True)]
  transfers between devices with their start and end apart: 3 -> 3, of which waited for: 3 -> 3; matrix products, arithmetic and copies ran while one was open for 5% -> 3% of each run, Pallas kernels for 0% -> 0%
where the time goes in v1:
time: 551 us; the launch traced here: 549 us
  waiting for transfers between devices  401 us (73%)
  starting transfers between devices  48.3 us (9%)
  local copies, waits for them, and re-layouts  36.6 us (7%)
  matrix products  33.5 us (6%)
  other arithmetic  26 us (5%)
    all_to_all x1, waiting for transfers between devices, tiled_gather(): lax.all_to_all(jnp.tile(array, repeats), axis, split_axis=dim, concat_axi...  196 us
    all_to_all x1, waiting for transfers between devices, body(): lax.all_to_all(shaped_parts, 'blk', split_axis=1, concat_axis=1, tiled=True)  187 us
    all_to_all x1, starting transfers between devices, tiled_gather(): lax.all_to_all(jnp.tile(array, repeats), axis, split_axis=dim, concat_axi...  34.5 us
    dot_general x4, matrix products, shard_partial(): jnp.einsum('bkgrs,bskd->bkgrd', weights.astype(jnp.bfloat16), value_split...  21.7 us
    all_to_all x1, waiting for transfers between devices, body(): lax.all_to_all(shaped_logs, 'blk', split_axis=1, concat_axis=1, tiled=True)  17.5 us
    reduce_sum x4, other arithmetic, shard_partial(): totals = jnp.sum(weights, axis=-1)  17.2 us
    dot_general x4, matrix products, shard_partial(): jnp.einsum('brkgd,bskd->bkgrs', query_split, key_split, preferred_element...  11.8 us
  transfers between devices with their start and end apart: 3, of which 3 were waited for; matrix products, arithmetic and copies ran while one was open for 3% of the time, Pallas kernels for 0%

profile of v1, /device:TPU:37, one launch (start us, length us, event | category | flops | bytes accessed | tf_op | source)
XLA Modules:
  0.0 548.6 jit_solution(2496622524709183026)
XLA Ops:
  0.0 0.9 copy.51
  0.9 3.4 tile.4
  4.3 34.5 %all-to-all-start = ((bf16[2,256,2048]{2,0,1:T(2,128)(2,1)}), bf16[2,256,2048]{2,0,1:T(2,128)(2,1)}, u32[]{:S(2)}, u32[]{:S(2)}) async-start(bf16[2,256,2048]{2,0,1:T(2,128)(2,1)} %bitcast), calls=%async_computation | async-start | bytes 4194304 | tf_op jit(solution)/shard_map/all_to_all | solution.py:15
  38.8 1.2 reshape.101
  40.4 195.8 %all-to-all-done = bf16[2,256,2048]{2,0,1:T(2,128)(2,1)} async-done(((bf16[2,256,2048]{2,0,1:T(2,128)(2,1)}), bf16[2,256,2048]{2,0,1:T(2,128)(2,1)}, u32[]{:S(2)}, u32[]{:S(2)}) %all-to-all-start) | async-done | bytes 2097184 | tf_op jit(solution)/shard_map/all_to_all | solution.py:15
  236.2 71.9 %while.14 = (s32[]{:T(128)}, bf16[4,2,64,2048]{3,2,1,0:T(8,128)(2,1)}, f32[4,2,64,16]{2,3,1,0:T(8,128)S(1)}, s32[4]{0:T(128)S(1)}, s32[2]{0:T(128)S(1)}, /*index...) while((s32[]{:T(128)}, ...), condition=%wide.wide.region_4.5_spmd.clone, body=%wide.wide.region_0.4_spmd.clone.sunk | while | flops 1377611520 | bytes 88389816 | solution.py:76
  237.6 1.4 constant_dynamic-slice_fusion.3
  239.7 3.0 fusion.38
  243.1 4.3 fusion.39
  247.6 5.4 divide_convert_fusion.4
  253.4 0.9 constant_dynamic-update-slice_fusion.3
  255.6 1.4 constant_dynamic-slice_fusion.3
  257.7 3.0 fusion.38
  261.0 4.3 fusion.39
  265.6 5.4 divide_convert_fusion.4
  271.4 0.9 constant_dynamic-update-slice_fusion.3
  273.6 1.4 constant_dynamic-slice_fusion.3
  275.7 3.0 fusion.38
  279.0 4.3 fusion.39
  283.6 5.4 divide_convert_fusion.4
  291.5 1.4 constant_dynamic-slice_fusion.3
  293.6 3.0 fusion.38
  297.0 4.3 fusion.39
  301.5 5.4 divide_convert_fusion.4
  309.1 7.8 %all-to-all-start.2 = ((f32[64,1,128]{2,1,0:T(1,128)}), f32[64,1,128]{2,1,0:T(1,128)S(1)}, u32[]{:S(2)}, u32[]{:S(2)}) async-start(f32[64,1,128]{2,1,0:T(1,128)} %reshape.99), calls=%async_computation.2 | async-start | bytes 65536 | tf_op jit(solution)/shard_map/all_to_all | solution.py:85
  317.0 5.1 copy.53
  322.1 17.5 %all-to-all-done.2 = f32[64,1,128]{2,1,0:T(1,128)S(1)} async-done(((f32[64,1,128]{2,1,0:T(1,128)}), f32[64,1,128]{2,1,0:T(1,128)S(1)}, u32[]{:S(2)}, u32[]{:S(2)}) %all-to-all-start.2) | async-done | bytes 32800 | tf_op jit(solution)/shard_map/all_to_all | solution.py:85
  339.6 6.0 %all-to-all-start.1 = ((bf16[2,64,4,2048]{3,0,2,1:T(2,128)(2,1)}), bf16[2,64,4,2048]{3,0,2,1:T(2,128)(2,1)S(1)}, u32[]{:S(2)}, u32[]{:S(2)}) async-start(bf16[2,64,4,2048]{3,0,2,1:T(2,128)(2,1)} %bitcast.94), calls=%async_computation.1 | async-start | bytes 4194304 | tf_op jit(solution)/shard_map/all_to_all | solution.py:84
  347.5 2.6 mul.27
  350.1 5.8 %mul.28 = f32[2,64,4,2048]{3,0,2,1:T(2,128)} reshape(f32[2,64,4,16,128]{4,3,0,2,1:T(8,128)} %mul.27) | data formatting | bytes 8388608 | tf_op jit(solution)/shard_map/mul | solution.py:90
  356.0 187.4 %all-to-all-done.1 = bf16[2,64,4,2048]{3,0,2,1:T(2,128)(2,1)S(1)} async-done(((bf16[2,64,4,2048]{3,0,2,1:T(2,128)(2,1)}), bf16[2,64,4,2048]{3,0,2,1:T(2,128)(2,1)S(1)}, u32[]{:S(2)}, u32[]{:S(2)}) %all-to-all-start.1) | async-done | bytes 2097184 | tf_op jit(solution)/shard_map/all_to_all | solution.py:84
  543.4 4.5 multiply_reduce_fusion
  (104 shorter events, 14.4 us)
Async XLA Ops:
  0.0 38.8 %copy-start.2 = (bf16[2,1280,256]{2,1,0:T(8,128)(2,1)S(1)}, bf16[2,1280,256]{2,1,0:T(8,128)(2,1)}, u32[]{:S(2)}) copy-start(bf16[2,1280,256]{2,1,0:T(8,128)(2,1)} %param.9) | copy-start | bytes 3932164
  0.9 39.2 %copy-start.1 = (bf16[2,1280,256]{2,1,0:T(8,128)(2,1)S(1)}, bf16[2,1280,256]{2,1,0:T(8,128)(2,1)}, u32[]{:S(2)}) copy-start(bf16[2,1280,256]{2,1,0:T(8,128)(2,1)} %param.8) | copy-start | bytes 3932164
  4.3 232.0 %copy-start.4 = (s32[2]{0:T(128)S(1)}, s32[2]{0:T(128)}, u32[]{:S(2)}) copy-start(s32[2]{0:T(128)} %param.10) | copy-start | bytes 28
  4.3 232.0 %copy-start.5 = (s32[2]{0:T(128)S(1)}, s32[2]{0:T(128)}, u32[]{:S(2)}) copy-start(s32[2]{0:T(128)} %param.11) | copy-start | bytes 28
  4.3 231.9 %all-to-all-start = ((bf16[2,256,2048]{2,0,1:T(2,128)(2,1)}), bf16[2,256,2048]{2,0,1:T(2,128)(2,1)}, u32[]{:S(2)}, u32[]{:S(2)}) async-start(bf16[2,256,2048]{2,0,1:T(2,128)(2,1)} %bitcast), calls=%async_computation | async-start | bytes 4194304 | tf_op jit(solution)/shard_map/all_to_all | solution.py:15
  242.7 4.7 copy-start
  243.1 4.5 copy-start.3
  260.7 4.7 copy-start
  261.0 4.5 copy-start.3
  278.7 4.7 copy-start
  279.0 4.5 copy-start.3
  296.6 4.7 copy-start
  297.0 4.5 copy-start.3
  309.1 30.5 %all-to-all-start.2 = ((f32[64,1,128]{2,1,0:T(1,128)}), f32[64,1,128]{2,1,0:T(1,128)S(1)}, u32[]{:S(2)}, u32[]{:S(2)}) async-start(f32[64,1,128]{2,1,0:T(1,128)} %reshape.99), calls=%async_computation.2 | async-start | bytes 65536 | tf_op jit(solution)/shard_map/all_to_all | solution.py:85
  339.6 203.8 %all-to-all-start.1 = ((bf16[2,64,4,2048]{3,0,2,1:T(2,128)(2,1)}), bf16[2,64,4,2048]{3,0,2,1:T(2,128)(2,1)S(1)}, u32[]{:S(2)}, u32[]{:S(2)}) async-start(bf16[2,64,4,2048]{3,0,2,1:T(2,128)(2,1)} %bitcast.94), calls=%async_computation.1 | async-start | bytes 4194304 | tf_op jit(solution)/shard_map/all_to_all | solution.py:84
